TPU v7x, 8 devices: a whole 2x2x1 slice. The times are simulated.
8 devices in a mesh: dp: 1 (over z), tp: 8 (over y, x, core).
Axes of the slice: x: 2, y: 2, z: 1, core: 2. Of those that a mesh axis runs over, the one named last changes fastest.
Arguments:
- x: bfloat16 [512, 2048], P('dp')
- k_cache: bfloat16 [512, 64, 16, 128], P('dp', None, 'tp')
- v_cache: bfloat16 [512, 64, 16, 128], P('dp', None, 'tp')
- positions: int32 [512], P('dp')
- att_ids: int32 [512, 2], P('dp')
- mlp_ids: int32 [512, 2], P('dp')
- norm_att: float32 [2048], replicated
- w_kv: bfloat16 [2048, 16, 256], P(None, 'tp')
- router_att: bfloat16 [2048, 8], replicated
- w_query: bfloat16 [8, 2048, 2048], P(None, None, 'tp')
- w_out: bfloat16 [8, 2048, 2048], P(None, 'tp')
- norm_mlp: float32 [2048], replicated
- router_mlp: bfloat16 [2048, 8], replicated
- w_gate: bfloat16 [8, 2048, 5632], P('tp')
- w_up: bfloat16 [8, 2048, 5632], P('tp')
- w_down: bfloat16 [8, 5632, 2048], P('tp')
Outputs:
- output 1: bfloat16 [512, 2048], P('dp')
- output 2: bfloat16 [512, 64, 16, 128], P('dp', None, 'tp')
- output 3: bfloat16 [512, 64, 16, 128], P('dp', None, 'tp')
All inputs are finite; a program needn't handle non-finite values.
Results may differ from a plain program's by a relative error of at most 0.012683.
Values are sent between devices in bfloat16 or wider.
A program may use at most 1 GiB of HBM per device.

v0:
```python
import jax
import jax.numpy as jnp
from jax import lax
from jax.sharding import PartitionSpec as P

NORM_EPS = 1e-6
ROPE_BASE = 10000.0


def rms_norm(x, gain):
    values = x.astype(jnp.float32)
    inv_rms = lax.rsqrt(jnp.mean(values * values, axis=-1, keepdims=True) + NORM_EPS)
    return (values * inv_rms * gain).astype(jnp.bfloat16)


def rope_tables(positions, head_dim):
    half_dim = head_dim // 2
    inv_freq = ROPE_BASE ** (-(jnp.arange(half_dim, dtype=jnp.float32) * 2.0 / head_dim))
    angles = positions.astype(jnp.float32)[:, None] * inv_freq[None, :]
    return jnp.cos(angles), jnp.sin(angles)


def apply_rope(vectors, cos_table, sin_table):
    half_dim = vectors.shape[-1] // 2
    first_half = vectors[..., :half_dim]
    second_half = vectors[..., half_dim:]
    return jnp.concatenate([first_half * cos_table - second_half * sin_table, second_half * cos_table + first_half * sin_table], axis=-1)


def route_weights(logits, choice_ids, first_id, count):
    pair_gates = jax.nn.softmax(jnp.take_along_axis(logits, choice_ids, axis=1), axis=-1)
    expert_index = first_id + jnp.arange(count)
    onehot = (choice_ids[:, :, None] == expert_index[None, None, :]).astype(jnp.float32)
    dense_gates = jnp.sum(onehot * pair_gates[:, :, None], axis=1)
    return onehot, dense_gates


def attention_part(hidden, k_cache, v_cache, positions, att_ids, w_kv, router_att, w_query, w_out):
    tokens = hidden.shape[0]
    head_count = k_cache.shape[2]
    head_dim = k_cache.shape[3]
    kv_new = jnp.einsum('bd,dnc->bnc', hidden, w_kv, preferred_element_type=jnp.float32)
    cos_table, sin_table = rope_tables(positions, head_dim)
    key_new = apply_rope(kv_new[:, :, :head_dim], cos_table[:, None, :], sin_table[:, None, :]).astype(jnp.bfloat16)
    value_new = kv_new[:, :, head_dim:].astype(jnp.bfloat16)
    slot_index = jnp.arange(k_cache.shape[1])
    at_slot = (slot_index[None, :] == positions[:, None])[:, :, None, None]
    keys_all = jnp.where(at_slot, key_new[:, None, :, :], k_cache)
    values_all = jnp.where(at_slot, value_new[:, None, :, :], v_cache)
    att_logits = jnp.dot(hidden, router_att, preferred_element_type=jnp.float32)
    att_onehot, att_dense = route_weights(att_logits, att_ids, 0, w_query.shape[0])
    query_all = jnp.einsum('bd,edc->bec', hidden, w_query, preferred_element_type=jnp.float32)
    query_sel = jnp.take_along_axis(query_all, att_ids[:, :, None], axis=1).reshape(tokens, 2, head_count, head_dim)
    query_rot = apply_rope(query_sel, cos_table[:, None, None, :], sin_table[:, None, None, :]).astype(jnp.bfloat16)
    scores = jnp.einsum('bknd,bsnd->bkns', query_rot, keys_all, preferred_element_type=jnp.float32) * head_dim ** -0.5
    visible = (slot_index[None, :] <= positions[:, None])[:, None, None, :]
    weights = jax.nn.softmax(jnp.where(visible, scores, -1e30), axis=-1).astype(jnp.bfloat16)
    attended = jnp.einsum('bkns,bsnd->bknd', weights, values_all, preferred_element_type=jnp.float32).astype(jnp.bfloat16).reshape(tokens, 2, head_count * head_dim)
    out_slots = jnp.einsum('bke,bkc->bec', att_onehot.astype(jnp.bfloat16), attended, preferred_element_type=jnp.float32).astype(jnp.bfloat16)
    projected = jnp.einsum('bec,ecd->bed', out_slots, w_out, preferred_element_type=jnp.float32)
    att_part = jnp.sum(att_dense[:, :, None] * projected, axis=1)
    return att_part, keys_all, values_all


def expert_part(normed, mlp_dense, w_gate, w_up, w_down):
    gate_val = jnp.einsum('bd,edf->bef', normed, w_gate, preferred_element_type=jnp.float32)
    up_val = jnp.einsum('bd,edf->bef', normed, w_up, preferred_element_type=jnp.float32)
    activation = (jax.nn.silu(gate_val) * up_val).astype(jnp.bfloat16)
    down_out = jnp.einsum('bef,efd->bed', activation, w_down, preferred_element_type=jnp.float32)
    return jnp.sum(mlp_dense[:, :, None] * down_out, axis=1)


def solution(mesh):
    def local_step(x, k_cache, v_cache, positions, att_ids, mlp_ids, norm_att, w_kv, router_att, w_query, w_out, norm_mlp, router_mlp, w_gate, w_up, w_down):
        hidden = rms_norm(x, norm_att)
        att_part, keys_all, values_all = attention_part(hidden, k_cache, v_cache, positions, att_ids, w_kv, router_att, w_query, w_out)
        att_sum = lax.psum(att_part.astype(jnp.bfloat16), 'tp').astype(jnp.float32)
        x_mid = (x.astype(jnp.float32) + att_sum).astype(jnp.bfloat16)
        normed = rms_norm(x_mid, norm_mlp)
        mlp_logits = jnp.dot(normed, router_mlp, preferred_element_type=jnp.float32)
        local_count = w_gate.shape[0]
        _, mlp_dense = route_weights(mlp_logits, mlp_ids, lax.axis_index('tp') * local_count, local_count)
        mlp_part = expert_part(normed, mlp_dense, w_gate, w_up, w_down)
        mlp_sum = lax.psum(mlp_part.astype(jnp.bfloat16), 'tp').astype(jnp.float32)
        x_out = (x_mid.astype(jnp.float32) + mlp_sum).astype(jnp.bfloat16)
        return x_out, keys_all, values_all

    token_spec = P('dp', None)
    cache_spec = P('dp', None, 'tp', None)
    expert_spec = P('tp', None, None)
    in_specs = (token_spec, cache_spec, cache_spec, P('dp'), token_spec, token_spec, P(), P(None, 'tp', None), P(), P(None, None, 'tp'), P(None, 'tp', None), P(), P(), expert_spec, expert_spec, expert_spec)
    out_specs = (token_spec, cache_spec, cache_spec)
    return jax.shard_map(local_step, mesh=mesh, in_specs=in_specs, out_specs=out_specs, check_vma=False)
```

profile of v0, /device:TPU:0, one launch (start us, length us, event | category | flops | bytes accessed | tf_op | source)
XLA Modules:
  0.0 327.0 jit_solution(15009062020723945117)
XLA Ops:
  7.2 0.8 convert_element_type.75
  8.9 2.1 fusion.14
  11.0 3.0 fusion.34
  15.4 2.3 fusion.68
  18.0 6.7 %gather_fusion.1 = f32[1024]{0:T(1024)S(1)} fusion(f32[512,8]{0,1:T(8,128)S(1)} %fusion.68, s32[1024]{0:T(1024)S(1)} %reshape.273), kind=kCustom, calls=%fused_computation.clone | custom fusion | bytes 16384 | tf_op jit(solution)/shard_map/jit(take_along_axis)/gather | solution.py:31
  25.3 7.7 %fusion.32 = f32[512,8,256]{2,0,1:T(8,128)S(1)} fusion(bf16[8,2048,256]{2,1,0:T(8,128)(2,1)} %param.27, bf16[512,2048]{1,0:T(8,128)(2,1)} %param.18, f32[2048]{0:T(1024)S(1)} %copy-done.10, f32[512]{0:T(512)S(1)} %add_rsqrt_fusion.1), kind=kOutput, calls=%fused_computation.36 | convolution fusion | flops 4299161600 | bytes 14690304 | tf_op jit(solution)/shard_map/bd,edc->bec/dot_general | solution.py:52
  33.0 4.4 %copy.93 = f32[512,8,256]{2,1,0:T(8,128)} copy(f32[512,8,256]{2,0,1:T(8,128)S(1)} %fusion.32) | data formatting | bytes 8388608 | tf_op jit(solution)/shard_map/bd,edc->bec/dot_general | solution.py:52
  37.4 12.0 %gather_fusion = f32[1024,256]{1,0:T(8,128)S(1)} fusion(f32[512,8,256]{2,1,0:T(8,128)} %copy.93, s32[1024]{0:T(1024)S(1)} %reshape.273), kind=kCustom, calls=%fused_computation.2 | custom fusion | bytes 2105344 | tf_op jit(solution)/shard_map/jit(take_along_axis)/gather | solution.py:53
  50.0 0.9 copy.99
  50.9 2.6 copy_select_fusion
  53.5 1.7 subtract_convert_fusion
  55.2 44.6 %broadcast_select_fusion = (bf16[512,64,2,128]{3,2,1,0:T(2,128)(2,1)}, bf16[512,64,2,128]{3,2,1,0:T(2,128)(2,1)}) fusion(bf16[512,64,2,128]{3,2,1,0:T(2,128)(2,1)} %param.19, pred[512,64]{1,0:T(8,128)(4,1)S(1)} %get-tuple-element.17, bf16[512,2,128]{2,1,0:T(2,128)(2,1)S(1)} %copy.90, bf16[512,64,2,128]{3,2,1,0:T(2,128)(2,1)} %param.20, ...), kind=kLoop, calls=%fused_computation.6 | loop fusion | flops 16777216 | bytes 67665920 | tf_op jit(solution)/shard_map/jit(_where)/select_n | solution.py:48
  99.8 13.5 %fusion.71 = (f32[512,2,2]{1,2,0:T(2,128)S(1)}, f32[512,2,2,64]{3,1,2,0:T(2,128)S(1)}) fusion(pred[512,64]{1,0:T(8,128)(4,1)S(1)} %get-tuple-element.16, bf16[512,64,2,128]{3,2,1,0:T(2,128)(2,1)} %get-tuple-element.12, bf16[512,2,2,64]{3,1,2,0:T(2,128)(2,1)S(1)} %get-tuple-element.9, bf16[512,2,2,64]{3,1,2,0:T(2,128)(2,1)S(1)} %get-tuple-element.8), kind=kOutput, calls=%fused_computation.93 | convolution fusion | flops 35127360 | bytes 17866752 | tf_op jit(solution)/shard_map/sub | solution.py:57
  113.4 13.4 %convolution_convert_fusion = bf16[512,8,256]{2,1,0:T(8,128)(2,1)} fusion(bf16[512,2,8]{2,1,0:T(2,128)(2,1)S(1)} %copy-done.4, bf16[512,64,2,128]{3,2,1,0:T(2,128)(2,1)} %get-tuple-element.13, f32[512,2,2,64]{3,1,2,0:T(2,128)S(1)} %get-tuple-element.19, f32[512,2,2]{1,2,0:T(2,128)S(1)} %get-tuple-element.18), kind=kOutput, calls=%fused_computation.42 | convolution fusion | flops 39321600 | bytes 19423232 | tf_op jit(solution)/shard_map/bke,bkc->bec/dot_general | solution.py:59
  126.8 11.7 %fusion.1 = bf16[512,2048]{1,0:T(8,128)(2,1)} fusion(bf16[8,256,2048]{2,1,0:T(8,128)(2,1)} %param.28, f32[512,8]{0,1:T(8,128)S(1)} %select_reduce_fusion, bf16[512,8,256]{2,1,0:T(8,128)(2,1)} %convolution_convert_fusion), kind=kOutput, calls=%fused_computation.5 | convolution fusion | flops 4310695936 | bytes 12599296 | tf_op jit(solution)/shard_map/bec,ecd->bed/dot_general | solution.py:60
  139.0 52.6 %all-reduce.3.cloned.1.call-done = bf16[512,2048]{1,0:T(8,128)(2,1)} async-done(((bf16[512,2048]{1,0:T(8,128)(2,1)}), bf16[512,2048]{1,0:T(8,128)(2,1)}) %all-reduce.3.cloned.1.call-update) | async-done | bytes 2097168 | tf_op jit(solution)/shard_map/psum | solution.py:77
  191.6 3.1 fusion.18
  194.7 2.6 fusion.20
  197.4 19.8 %fusion.6 = f32[512,5632]{1,0:T(8,128)} fusion(bf16[512,2048]{1,0:T(8,128)(2,1)S(1)} %fusion.20, bf16[1,2048,5632]{2,1,0:T(8,128)(2,1)} %param.31), kind=kOutput, calls=%fused_computation.12 | convolution fusion | flops 11811160064 | bytes 36700160 | tf_op jit(solution)/shard_map/bd,edf->bef/dot_general | solution.py:66
  217.9 6.5 %gather_fusion.2 = f32[1024]{0:T(1024)S(1)} fusion(f32[512,8]{0,1:T(8,128)S(1)} %fusion.80, s32[1024]{0:T(1024)S(1)} %reshape.278), kind=kCustom, calls=%fused_computation.1.clone | custom fusion | bytes 16384 | tf_op jit(solution)/shard_map/jit(take_along_axis)/gather | solution.py:31
  224.8 20.7 %multiply_convert_fusion.clone.6 = bf16[512,5632]{1,0:T(8,128)(2,1)} fusion(f32[512,5632]{1,0:T(8,128)} %fusion.6, bf16[512,2048]{1,0:T(8,128)(2,1)} %copy-done.3, bf16[1,2048,5632]{2,1,0:T(8,128)(2,1)} %param.32), kind=kOutput, calls=%fused_computation.18.clone.clone.clone.clone.clone.1 | convolution fusion | flops 11828461568 | bytes 42467328 | tf_op jit(solution)/shard_map/bd,edf->bef/dot_general | solution.py:67
  245.6 19.3 %fusion.27 = bf16[512,2048]{1,0:T(8,128)(2,1)} fusion(bf16[1,5632,2048]{2,1,0:T(8,128)(2,1)} %param.33, f32[512]{0:T(512)S(1)} %fusion.59, bf16[512,5632]{1,0:T(8,128)(2,1)} %multiply_convert_fusion.clone.6), kind=kOutput, calls=%fused_computation.35 | convolution fusion | flops 11813257216 | bytes 30935040 | tf_op jit(solution)/shard_map/bef,efd->bed/dot_general | solution.py:69
  264.9 49.4 %all-reduce.5.cloned.1.call-done = bf16[512,2048]{1,0:T(8,128)(2,1)} async-done(((bf16[512,2048]{1,0:T(8,128)(2,1)}), bf16[512,2048]{1,0:T(8,128)(2,1)}) %all-reduce.5.cloned.1.call-update) | async-done | bytes 2097168 | tf_op jit(solution)/shard_map/psum | solution.py:84
  314.3 5.6 %fusion.21 = bf16[512,2048]{1,0:T(8,128)(2,1)} fusion(bf16[512,2048]{1,0:T(8,128)(2,1)} %all-reduce.5.cloned.1.call-done, bf16[512,2048]{1,0:T(8,128)(2,1)} %all-reduce.3.cloned.1.call-done, bf16[512,2048]{1,0:T(8,128)(2,1)} %param.18), kind=kLoop, calls=%fused_computation.32 | loop fusion | flops 8388608 | bytes 8388608 | tf_op jit(solution)/shard_map/convert_element_type | solution.py:85
  (59 shorter events, 5.1 us)
Async XLA Ops:
  7.2 3.8 %copy-start = (bf16[2048,2,256]{2,1,0:T(2,128)(2,1)S(1)}, bf16[2048,2,256]{2,1,0:T(2,128)(2,1)}, u32[]{:S(2)}) copy-start(bf16[2048,2,256]{2,1,0:T(2,128)(2,1)} %param.25) | copy-start | bytes 6291460
  7.2 184.4 %all-reduce.3.cloned.1.call-start = ((), (), s32[]{:S(2)}) async-start(), calls=%async_computation | async-start | bytes 4194304 | tf_op jit(solution)/shard_map/psum | solution.py:77
  11.0 4.0 %copy-start.5 = (s32[512,2]{0,1:T(2,128)S(1)}, s32[512,2]{0,1:T(2,128)}, u32[]{:S(2)}) copy-start(s32[512,2]{0,1:T(2,128)} %param.22) | copy-start | bytes 12292
  14.0 1.4 copy-start.9
  14.0 1.4 copy-start.10
  99.8 13.6 %copy-start.4 = (bf16[512,2,8]{2,1,0:T(2,128)(2,1)S(1)}, bf16[512,2,8]{2,1,0:T(2,128)(2,1)}, u32[]{:S(2)}) copy-start(bf16[512,2,8]{2,1,0:T(2,128)(2,1)} %copy.99) | copy-start | bytes 49156
  126.8 11.8 %copy-start.6 = (s32[512,2]{0,1:T(2,128)S(1)}, s32[512,2]{0,1:T(2,128)}, u32[]{:S(2)}) copy-start(s32[512,2]{0,1:T(2,128)} %param.23) | copy-start | bytes 12292
  138.5 56.2 %copy-start.8 = (f32[2048]{0:T(1024)S(1)}, f32[2048]{0:T(1024)}, u32[]{:S(2)}) copy-start(f32[2048]{0:T(1024)} %param.29) | copy-start | bytes 24580
  138.6 175.8 %all-reduce.5.cloned.1.call-start = ((), (), s32[]{:S(2)}) async-start(), calls=%async_computation.1 | async-start | bytes 4194304 | tf_op jit(solution)/shard_map/psum | solution.py:84
  191.6 3.1 copy-start.2
  197.4 19.9 %copy-start.3 = (bf16[512,2048]{1,0:T(8,128)(2,1)}, bf16[512,2048]{1,0:T(8,128)(2,1)S(1)}, u32[]{:S(2)}) copy-start(bf16[512,2048]{1,0:T(8,128)(2,1)S(1)} %fusion.20) | copy-start | bytes 6291460
  197.4 19.9 %copy-start.7 = (bf16[2048,8]{0,1:T(8,128)(2,1)S(1)}, bf16[2048,8]{0,1:T(8,128)(2,1)}, u32[]{:S(2)}) copy-start(bf16[2048,8]{0,1:T(8,128)(2,1)} %param.30) | copy-start | bytes 98308
  264.9 55.0 %copy-start.1 = (bf16[2048,2,256]{2,1,0:T(2,128)(2,1)S(1)}, bf16[2048,2,256]{2,1,0:T(2,128)(2,1)}, u32[]{:S(2)}) copy-start(bf16[2048,2,256]{2,1,0:T(2,128)(2,1)} %param.25) | copy-start | bytes 6291460
Sparse Core Ops, SparseCore 0:
  138.7 52.8 all-reduce.2
  265.0 49.2 all-reduce.4
where the time goes:
time: 331 us; the launch traced here: 327 us
  matrix products  112 us (34%)
  waiting for transfers between devices  102 us (31%)
  other arithmetic  64.9 us (20%)
  local copies, waits for them, and re-layouts  33.2 us (10%)
  between operations  14.6 us (4%)
    psum x1, waiting for transfers between devices, local_step(): att_sum = lax.psum(att_part.astype(jnp.bfloat16), 'tp').astype(jnp.float32)  52.6 us
    psum x1, waiting for transfers between devices, local_step(): mlp_sum = lax.psum(mlp_part.astype(jnp.bfloat16), 'tp').astype(jnp.float32)  49.4 us
    select_n x1, other arithmetic, attention_part(): keys_all = jnp.where(at_slot, key_new[:, None, :, :], k_cache)  44.6 us
    dot_general x1, matrix products, expert_part(): jnp.einsum('bd,edf->bef', normed, w_up, preferred_element_type=jnp.float32)  20.7 us
    dot_general x1, matrix products, expert_part(): jnp.einsum('bd,edf->bef', normed, w_gate, preferred_element_type=jnp.floa...  19.8 us
    dot_general x1, matrix products, expert_part(): jnp.einsum('bef,efd->bed', activation, w_down, preferred_element_type=jnp...  19.3 us
    gather x10, local copies, waits for them, and re-layouts, route_weights(): jnp.take_along_axis(logits, choice_ids, axis=1)  14.5 us
    sub x1, matrix products, attention_part(): jax.nn.softmax(jnp.where(visible, scores, -1e+30), axis=-1)  13.5 us
  transfers between devices with their start and end apart: 2, of which 2 were waited for; matrix products, arithmetic and copies ran while one was open for 0% of the time, Pallas kernels for 0%

commit v1 on v0

v1 whole, which is shorter than its diff:
```python
import functools

import jax
import jax.numpy as jnp
from jax import lax
from jax.experimental import pallas as pl
from jax.experimental.pallas import tpu as pltpu
from jax.sharding import PartitionSpec as P

NORM_EPS = 1e-6
ROPE_BASE = 10000.0
NEG = -1e30
VMEM_LIMIT = 60 * 1024 * 1024
ROW_SIZES = (256, 320, 384, 512)


def rms_rows(x, gain):
    values = x.astype(jnp.float32)
    inv_rms = lax.rsqrt(jnp.mean(values * values, axis=-1, keepdims=True) + NORM_EPS)
    return (values * inv_rms * gain).astype(jnp.bfloat16)


def project_kernel(x_ref, gain_ref, router_ref, ids_ref, cos_ref, sin_ref, wkv_ref, wq_ref, q_ref, k_ref, v_ref, gate_ref, h_ref, acc_ref):
    step = pl.program_id(0)
    experts = pl.num_programs(0)
    tokens = x_ref.shape[0]
    dim = cos_ref.shape[1]
    heads = k_ref.shape[0] // tokens

    def rope(vec):
        return vec * cos_ref[...] + pltpu.roll(vec, dim // 2, 1) * sin_ref[...]

    @pl.when(step == 0)
    def _():
        h_ref[...] = rms_rows(x_ref[...], gain_ref[...])
        acc_ref[...] = jnp.zeros_like(acc_ref)
        for n in range(heads):
            kv = jnp.dot(h_ref[...], wkv_ref[n], preferred_element_type=jnp.float32)
            k_ref[pl.ds(n, tokens, stride=heads), :] = rope(kv[:, :dim])
            v_ref[pl.ds(n, tokens, stride=heads), :] = kv[:, dim:]
        logits = lax.dot_general(h_ref[...], router_ref[...], (((1,), (1,)), ((), ())), preferred_element_type=jnp.float32)
        lane = lax.broadcasted_iota(jnp.int32, logits.shape, 1)
        is_first = lane == ids_ref[:, 0:1]
        is_second = lane == ids_ref[:, 1:2]
        first = jnp.sum(jnp.where(is_first, logits, 0.0), axis=1, keepdims=True)
        second = jnp.sum(jnp.where(is_second, logits, 0.0), axis=1, keepdims=True)
        top = jnp.maximum(first, second)
        e_first = jnp.exp(first - top)
        e_second = jnp.exp(second - top)
        total = e_first + e_second
        gate_ref[...] = jnp.where(is_first, e_first / total, 0.0) + jnp.where(is_second, e_second / total, 0.0)

    query = jnp.dot(h_ref[...], wq_ref[0], preferred_element_type=jnp.float32)
    for k in range(2):
        acc_ref[k] = jnp.where(ids_ref[:, k:k + 1] == step, query, acc_ref[k])

    @pl.when(step == experts - 1)
    def _():
        for k in range(2):
            for n in range(heads):
                q_ref[pl.ds(k * heads + n, tokens, stride=2 * heads), :] = rope(acc_ref[k, :, n * dim:(n + 1) * dim])


def project(x, gain, router_t, ids, cos, sin, w_kv, w_query):
    tokens, width = x.shape
    experts = w_query.shape[0]
    heads, dim = w_kv.shape[0], w_kv.shape[2] // 2
    full = lambda *shape: pl.BlockSpec(shape, lambda i: (0,) * len(shape))
    return pl.pallas_call(
        project_kernel,
        grid=(experts,),
        in_specs=[full(tokens, width), full(1, width), full(experts, width), full(tokens, 2), full(tokens, dim), full(tokens, dim),
                  full(heads, width, 2 * dim), pl.BlockSpec((1, width, heads * dim), lambda i: (i, 0, 0))],
        out_specs=[full(2 * heads * tokens, dim), full(heads * tokens, dim), full(heads * tokens, dim), full(tokens, experts)],
        out_shape=[jax.ShapeDtypeStruct((2 * heads * tokens, dim), jnp.float32), jax.ShapeDtypeStruct((heads * tokens, dim), jnp.float32),
                   jax.ShapeDtypeStruct((heads * tokens, dim), jnp.float32), jax.ShapeDtypeStruct((tokens, experts), jnp.float32)],
        scratch_shapes=[pltpu.VMEM((tokens, width), jnp.bfloat16), pltpu.VMEM((2, tokens, heads * dim), jnp.float32)],
        compiler_params=pltpu.CompilerParams(vmem_limit_bytes=VMEM_LIMIT),
        name='project',
    )(x, gain, router_t, ids, cos, sin, w_kv, w_query)


BLOCK = 32
SLOTS = 4
AHEAD = 2
GROUP = 2


def attend_kernel(pos_ref, q_ref, kn_ref, vn_ref, k_hbm, v_hbm, o_ref, ko_hbm, vo_hbm, kbuf, vbuf, in_sem, out_sem):
    tokens, rows, dim = k_hbm.shape
    blocks = tokens // BLOCK
    heads = kn_ref.shape[0] // tokens
    per_token = q_ref.shape[0] // tokens
    scale = dim ** -0.5

    def load(i, slot):
        span = pl.ds(i * BLOCK, BLOCK)
        return (pltpu.make_async_copy(k_hbm.at[span], kbuf.at[slot], in_sem.at[slot, 0]),
                pltpu.make_async_copy(v_hbm.at[span], vbuf.at[slot], in_sem.at[slot, 1]))

    def store(i, slot):
        span = pl.ds(i * BLOCK, BLOCK)
        return (pltpu.make_async_copy(kbuf.at[slot], ko_hbm.at[span], out_sem.at[slot, 0]),
                pltpu.make_async_copy(vbuf.at[slot], vo_hbm.at[span], out_sem.at[slot, 1]))

    for i in range(AHEAD):
        for copy in load(i, i):
            copy.start()

    tile_row = lax.broadcasted_iota(jnp.int32, (16, dim), 0)
    lanes = GROUP * rows
    q_rows = GROUP * per_token
    lane = lax.broadcasted_iota(jnp.int32, (q_rows, lanes), 1)
    row = lax.broadcasted_iota(jnp.int32, (q_rows, lanes), 0)
    match = (lane // rows == row // per_token) & (lane % heads == row % heads)
    slot_of = jnp.where(match, (lane % rows) // heads, rows)
    row_token = row // per_token

    def body(i, carry):
        slot = lax.rem(i, SLOTS)
        later = i + AHEAD

        @pl.when(later < blocks)
        def _():
            later_slot = lax.rem(later, SLOTS)

            @pl.when(later >= SLOTS)
            def _():
                for copy in store(later - SLOTS, later_slot):
                    copy.wait()
            for copy in load(later, later_slot):
                copy.start()

        for copy in load(i, slot):
            copy.wait()
        kb = kbuf.at[slot]
        vb = vbuf.at[slot]
        base_token = i * BLOCK
        positions = [pos_ref[base_token + t] for t in range(BLOCK)]
        for t in range(BLOCK):
            p = positions[t]
            start = pl.multiple_of((p // 8) * 16, 16)
            local = (p % 8) * heads
            for buf, new in ((kb, kn_ref), (vb, vn_ref)):
                tile = buf[t, pl.ds(start, 16), :].astype(jnp.float32)
                for n in range(heads):
                    tile = jnp.where(tile_row == local + n, new[pl.ds(heads * (base_token + t) + n, 1), :], tile)
                buf[t, pl.ds(start, 16), :] = tile.astype(jnp.bfloat16)
        for g in range(BLOCK // GROUP):
            first = (base_token + g * GROUP) * per_token
            q = q_ref[pl.ds(pl.multiple_of(first, q_rows), q_rows), :].astype(jnp.bfloat16)
            keys = kb[g * GROUP:(g + 1) * GROUP].reshape(lanes, dim)
            scores = lax.dot_general(q, keys, (((1,), (1,)), ((), ())), preferred_element_type=jnp.float32) * scale
            limit = positions[g * GROUP]
            for t in range(1, GROUP):
                limit = jnp.where(row_token == t, positions[g * GROUP + t], limit)
            scores = jnp.where(slot_of <= limit, scores, NEG)
            weights = jnp.exp(scores - jnp.max(scores, axis=1, keepdims=True))
            weights = (weights / jnp.sum(weights, axis=1, keepdims=True)).astype(jnp.bfloat16)
            values = vb[g * GROUP:(g + 1) * GROUP].reshape(lanes, dim)
            o_ref[pl.ds(pl.multiple_of(first, q_rows), q_rows), :] = jnp.dot(weights, values, preferred_element_type=jnp.float32)
        for copy in store(i, slot):
            copy.start()
        return carry

    lax.fori_loop(0, blocks, body, 0)
    for i in range(blocks - SLOTS, blocks):
        for copy in store(i, i % SLOTS):
            copy.wait()


def attend(positions, q, k_new, v_new, k_cache, v_cache):
    tokens, rows, dim = k_cache.shape
    vmem = pl.BlockSpec(memory_space=pltpu.VMEM)
    hbm = pl.BlockSpec(memory_space=pl.ANY)
    return pl.pallas_call(
        attend_kernel,
        in_specs=[pl.BlockSpec(memory_space=pltpu.SMEM), vmem, vmem, vmem, hbm, hbm],
        out_specs=[vmem, hbm, hbm],
        out_shape=[jax.ShapeDtypeStruct(q.shape, jnp.float32), jax.ShapeDtypeStruct(k_cache.shape, k_cache.dtype), jax.ShapeDtypeStruct(v_cache.shape, v_cache.dtype)],
        scratch_shapes=[pltpu.VMEM((SLOTS, BLOCK, rows, dim), jnp.bfloat16), pltpu.VMEM((SLOTS, BLOCK, rows, dim), jnp.bfloat16),
                        pltpu.SemaphoreType.DMA((SLOTS, 2)), pltpu.SemaphoreType.DMA((SLOTS, 2))],
        compiler_params=pltpu.CompilerParams(vmem_limit_bytes=VMEM_LIMIT),
        name='attend',
    )(positions, q, k_new, v_new, k_cache, v_cache)


def combine_kernel(o_ref, ids_ref, gate_ref, w_ref, out_ref, acc_ref):
    step = pl.program_id(0)
    experts = pl.num_programs(0)
    tokens = ids_ref.shape[0]
    per_token = o_ref.shape[0] // tokens
    heads = per_token // 2
    parts = []
    for n in range(heads):
        first = o_ref[pl.ds(n, tokens, stride=per_token), :]
        second = o_ref[pl.ds(heads + n, tokens, stride=per_token), :]
        parts.append(jnp.where(ids_ref[:, 0:1] == step, first, jnp.where(ids_ref[:, 1:2] == step, second, 0.0)).astype(jnp.bfloat16))
    rows = jnp.concatenate(parts, axis=1)
    projected = jnp.dot(rows, w_ref[0], preferred_element_type=jnp.float32)
    lane = lax.broadcasted_iota(jnp.int32, gate_ref.shape, 1)
    gate = jnp.sum(jnp.where(lane == step, gate_ref[...], 0.0), axis=1, keepdims=True)

    @pl.when(step == 0)
    def _():
        acc_ref[...] = gate * projected

    @pl.when((step > 0) & (step < experts - 1))
    def _():
        acc_ref[...] += gate * projected

    @pl.when(step == experts - 1)
    def _():
        out_ref[...] = (acc_ref[...] + gate * projected).astype(jnp.bfloat16)


def combine(o, ids, gates, w_out):
    experts, depth, width = w_out.shape
    tokens = ids.shape[0]
    full = lambda *shape: pl.BlockSpec(shape, lambda i: (0,) * len(shape))
    return pl.pallas_call(
        combine_kernel,
        grid=(experts,),
        in_specs=[full(*o.shape), full(tokens, 2), full(tokens, experts), pl.BlockSpec((1, depth, width), lambda i: (i, 0, 0))],
        out_specs=full(tokens, width),
        out_shape=jax.ShapeDtypeStruct((tokens, width), jnp.bfloat16),
        scratch_shapes=[pltpu.VMEM((tokens, width), jnp.float32)],
        compiler_params=pltpu.CompilerParams(vmem_limit_bytes=VMEM_LIMIT),
        name='combine',
    )(o, ids, gates, w_out)


def reduce_kernel(part_ref, base_ref, out_ref, pair_buf, send_buf, chip_buf, pair_send, pair_recv, chip_send, chip_recv, own_send, own_recv, fwd_send, fwd_recv):
    me = lax.axis_index('tp')
    rows = part_ref.shape[0] // 8
    core = me % 2
    x = (me // 2) % 2
    y = me // 4
    partner = me + 1 - 2 * core

    def chip(k):
        return 2 * ((y + k // 2) % 2) + (x + k % 2) % 2

    def span(device):
        return pl.ds(pl.multiple_of(device * rows, rows), rows)

    barrier = pltpu.get_barrier_semaphore()
    for device in [partner] + [2 * chip(k) + core for k in (1, 2, 3)]:
        pl.semaphore_signal(barrier, inc=1, device_id={'tp': device}, device_id_type=pl.DeviceIdType.MESH)
    pl.semaphore_wait(barrier, 4)

    def remote(src, dst, send, recv, device):
        return pltpu.make_async_remote_copy(src_ref=src, dst_ref=dst, send_sem=send, recv_sem=recv, device_id={'tp': device}, device_id_type=pl.DeviceIdType.MESH)

    order = (3, 1, 2, 0)
    pair = {}
    for k in order:
        pair[k] = remote(part_ref.at[span(2 * chip(k) + 1 - core)], pair_buf.at[k], pair_send.at[k], pair_recv.at[k], partner)
        pair[k].start()
    across = {}
    for k in order[:3]:
        pair[k].wait_recv()
        send_buf[k - 1] = (part_ref[span(2 * chip(k) + core), :].astype(jnp.float32) + pair_buf[k].astype(jnp.float32)).astype(jnp.bfloat16)
        across[k] = remote(send_buf.at[k - 1], chip_buf.at[k - 1], chip_send.at[k - 1], chip_recv.at[k - 1], 2 * chip(k) + core)
        across[k].start()
    pair[0].wait_recv()
    total = part_ref[span(me), :].astype(jnp.float32) + pair_buf[0].astype(jnp.float32)
    for k in (1, 2, 3):
        across[k].wait_recv()
        total = total + chip_buf[k - 1].astype(jnp.float32)
    out_ref[span(me), :] = (base_ref[span(me), :].astype(jnp.float32) + total).astype(jnp.bfloat16)

    own = {}
    for k in order[:3]:
        own[k] = remote(out_ref.at[span(me)], out_ref.at[span(me)], own_send.at[k], own_recv.at[k], 2 * chip(k) + core)
        own[k].start()
    forward = {0: remote(out_ref.at[span(me)], out_ref.at[span(me)], fwd_send.at[0], fwd_recv.at[0], partner)}
    forward[0].start()
    for k in (1, 2, 3):
        block = span(2 * chip(k) + core)
        own[k].wait_recv()
        forward[k] = remote(out_ref.at[block], out_ref.at[block], fwd_send.at[k], fwd_recv.at[k], partner)
        forward[k].start()
    for k in range(4):
        forward[k].wait_recv()
    for k in range(4):
        forward[k].wait_send()
        pair[k].wait_send()
    for k in (1, 2, 3):
        own[k].wait_send()
        across[k].wait_send()


def reduce_add(part, base, collective_id):
    tokens, width = part.shape
    rows = tokens // 8
    vmem = pl.BlockSpec(memory_space=pltpu.VMEM)
    return pl.pallas_call(
        reduce_kernel,
        in_specs=[vmem, vmem],
        out_specs=vmem,
        out_shape=jax.ShapeDtypeStruct((tokens, width), jnp.bfloat16),
        scratch_shapes=[pltpu.VMEM((4, rows, width), jnp.bfloat16), pltpu.VMEM((3, rows, width), jnp.bfloat16), pltpu.VMEM((3, rows, width), jnp.bfloat16)]
        + [pltpu.SemaphoreType.DMA((n,)) for n in (4, 4, 3, 3, 4, 4, 4, 4)],
        compiler_params=pltpu.CompilerParams(collective_id=collective_id, has_side_effects=True, vmem_limit_bytes=VMEM_LIMIT),
        name=f'reduce_{collective_id}',
    )(part, base)


def expert_kernel(first_ref, x_ref, gain_ref, router_ref, ids_ref, wg_ref, wu_ref, wd_ref, out_ref, rank_ref, gate_ref, rows_ref, acc_ref, count_ref):
    step = pl.program_id(0)
    steps = pl.num_programs(0)
    tokens, width = x_ref.shape
    experts = router_ref.shape[0]
    mine = first_ref[0]

    @pl.when(step == 0)
    def _():
        normed = rms_rows(x_ref[...], gain_ref[...])
        logits = lax.dot_general(router_ref[...], normed, (((1,), (1,)), ((), ())), preferred_element_type=jnp.float32)
        id_first = ids_ref[0:1, :]
        id_second = ids_ref[1:2, :]
        index = lax.broadcasted_iota(jnp.int32, (experts, tokens), 0)
        first = jnp.sum(jnp.where(index == id_first, logits, 0.0), axis=0, keepdims=True)
        second = jnp.sum(jnp.where(index == id_second, logits, 0.0), axis=0, keepdims=True)
        top = jnp.maximum(first, second)
        e_first = jnp.exp(first - top)
        e_second = jnp.exp(second - top)
        total = e_first + e_second
        gate = jnp.where(id_first == mine, e_first / total, 0.0) + jnp.where(id_second == mine, e_second / total, 0.0)
        chosen = (id_first == mine) | (id_second == mine)
        flags = jnp.where(chosen, 1.0, 0.0)
        below = (lax.broadcasted_iota(jnp.int32, (tokens, tokens), 0) <= lax.broadcasted_iota(jnp.int32, (tokens, tokens), 1)).astype(jnp.bfloat16)
        counts = jnp.dot(jnp.broadcast_to(flags, (8, tokens)).astype(jnp.bfloat16), below, preferred_element_type=jnp.float32)[0:1, :]
        rank = jnp.where(chosen, counts.astype(jnp.int32) - 1, -1)
        rank_ref[...] = rank
        count_ref[0] = jnp.sum(chosen.astype(jnp.int32))
        pick = lax.broadcasted_iota(jnp.int32, (tokens, tokens), 0) == rank
        gate_ref[...] = jnp.sum(jnp.where(pick, gate, 0.0), axis=1, keepdims=True)
        rows_ref[...] = jnp.dot(pick.astype(jnp.bfloat16), normed, preferred_element_type=jnp.float32).astype(jnp.bfloat16)

    def run(size):
        rows = rows_ref[:size, :]
        gate_val = jnp.dot(rows, wg_ref[0], preferred_element_type=jnp.float32)
        up_val = jnp.dot(rows, wu_ref[0], preferred_element_type=jnp.float32)
        act = (jax.nn.silu(gate_val) * up_val).astype(jnp.bfloat16)
        down = jnp.dot(act, wd_ref[0], preferred_element_type=jnp.float32)

        @pl.when(step == 0)
        def _():
            acc_ref[:size, :] = down

        @pl.when(step > 0)
        def _():
            acc_ref[:size, :] += down

        @pl.when(step == steps - 1)
        def _():
            mixed = (acc_ref[:size, :] * gate_ref[:size, :]).astype(jnp.bfloat16)
            pick = (lax.broadcasted_iota(jnp.int32, (size, tokens), 0) == rank_ref[...]).astype(jnp.bfloat16)
            out_ref[...] = lax.dot_general(pick, mixed, (((0,), (0,)), ((), ())), preferred_element_type=jnp.float32).astype(jnp.bfloat16)

    count = count_ref[0]
    lower = -1
    for size in ROW_SIZES:
        upper = size if size < tokens else tokens
        pl.when((count > lower) & (count <= upper))(functools.partial(run, size))
        lower = upper


def expert(first, x, gain, router_t, ids_t, w_gate, w_up, w_down):
    tokens, width = x.shape
    ffn = w_gate.shape[2]
    tile = 512
    full = lambda *shape: pl.BlockSpec(shape, lambda i: (0,) * len(shape))
    return pl.pallas_call(
        expert_kernel,
        grid=(ffn // tile,),
        in_specs=[pl.BlockSpec(memory_space=pltpu.SMEM), full(tokens, width), full(1, width), full(*router_t.shape), full(2, tokens),
                  pl.BlockSpec((1, width, tile), lambda i: (0, 0, i)), pl.BlockSpec((1, width, tile), lambda i: (0, 0, i)),
                  pl.BlockSpec((1, tile, width), lambda i: (0, i, 0))],
        out_specs=full(tokens, width),
        out_shape=jax.ShapeDtypeStruct((tokens, width), jnp.bfloat16),
        scratch_shapes=[pltpu.VMEM((1, tokens), jnp.int32), pltpu.VMEM((tokens, 1), jnp.float32), pltpu.VMEM((tokens, width), jnp.bfloat16),
                        pltpu.VMEM((tokens, width), jnp.float32), pltpu.SMEM((1,), jnp.int32)],
        compiler_params=pltpu.CompilerParams(vmem_limit_bytes=VMEM_LIMIT),
        name='expert',
    )(first, x, gain, router_t, ids_t, w_gate, w_up, w_down)


def solution(mesh):
    def local_step(x, k_cache, v_cache, positions, att_ids, mlp_ids, norm_att, w_kv, router_att, w_query, w_out, norm_mlp, router_mlp, w_gate, w_up, w_down):
        tokens, slots, heads, dim = k_cache.shape
        half = dim // 2
        inv_freq = ROPE_BASE ** (-(jnp.arange(half, dtype=jnp.float32) * 2.0 / dim))
        angles = positions.astype(jnp.float32)[:, None] * inv_freq[None, :]
        cos, sin = jnp.cos(angles), jnp.sin(angles)
        cos = jnp.concatenate([cos, cos], axis=1)
        sin = jnp.concatenate([-sin, sin], axis=1)
        q, k_new, v_new, gates = project(x, norm_att[None, :], router_att.T, att_ids, cos, sin, w_kv.transpose(1, 0, 2), w_query)
        merged = (tokens, slots * heads, dim)
        attended, keys_all, values_all = attend(positions, q, k_new, v_new, k_cache.reshape(merged), v_cache.reshape(merged))
        part = combine(attended, att_ids, gates, w_out)
        x_mid = reduce_add(part, x, 0)
        first = lax.axis_index('tp').reshape(1)
        mlp_part = expert(first, x_mid, norm_mlp[None, :], router_mlp.T, mlp_ids.T, w_gate, w_up, w_down)
        x_out = reduce_add(mlp_part, x_mid, 1)
        return x_out, keys_all.reshape(k_cache.shape), values_all.reshape(v_cache.shape)

    token_spec = P('dp', None)
    cache_spec = P('dp', None, 'tp', None)
    expert_spec = P('tp', None, None)
    in_specs = (token_spec, cache_spec, cache_spec, P('dp'), token_spec, token_spec, P(), P(None, 'tp', None), P(), P(None, None, 'tp'), P(None, 'tp', None), P(), P(), expert_spec, expert_spec, expert_spec)
    out_specs = (token_spec, cache_spec, cache_spec)
    return jax.shard_map(local_step, mesh=mesh, in_specs=in_specs, out_specs=out_specs, check_vma=False)
```

time: 331 us -> 242 us (0.73)
  Pallas kernels: 0 us -> 230 us
  matrix products: 112 us -> 0 us
  waiting for transfers between devices: 102 us -> 0 us
  other arithmetic: 64.9 us -> 2.68 us
  local copies, waits for them, and re-layouts: 33.2 us -> 7.87 us
  between operations: 14.6 us -> 0.67 us
    pallas_call x0 -> x6, Pallas kernels: none -> 230 us  [the longest x1 91.1 us: attend(): pl.pallas_call(attend_kernel, in_specs=[pl.BlockSpec(memory_space=pltpu.S...]
    psum x2 -> x0, waiting for transfers between devices: 102 us -> none  [the longest x1 52.6 us: local_step(): att_sum = lax.psum(att_part.astype(jnp.bfloat16), 'tp').astype(jnp.float32)]
    dot_general x9 -> x0, matrix products: 98.6 us -> none  [the longest x1 20.7 us: expert_part(): jnp.einsum('bd,edf->bef', normed, w_up, preferred_element_type=jnp.float32)]
    select_n x2 -> x0, other arithmetic: 47.2 us -> none  [the longest x1 44.6 us: attention_part(): keys_all = jnp.where(at_slot, key_new[:, None, :, :], k_cache)]
    gather x12 -> x0, local copies, waits for them, and re-layouts: 27 us -> none  [the longest x10 14.5 us: route_weights(): jnp.take_along_axis(logits, choice_ids, axis=1)]
    sub x1 -> x0, matrix products: 13.5 us -> none  [attention_part(): jax.nn.softmax(jnp.where(visible, scores, -1e+30), axis=-1)]
    convert_element_type x4 -> x1, other arithmetic: 9.06 us -> 0.69 us  [local_step(): angles = positions.astype(jnp.float32)[:, None] * inv_freq[None, :]]
    unnamed x22 -> x3, local copies, waits for them, and re-layouts: 0.07 us -> 7.87 us
  transfers between devices with their start and end apart: 2 -> 0, of which waited for: 2 -> 0; matrix products, arithmetic and copies ran while one was open for 0% -> 0% of each run, Pallas kernels for 0% -> 0%
where the time goes in v1:
time: 242 us; the launch traced here: 241 us
  Pallas kernels  230 us (95%)
  local copies, waits for them, and re-layouts  7.87 us (3%)
  other arithmetic  2.68 us (1%)
    pallas_call x1, Pallas kernels, attend(): pl.pallas_call(attend_kernel, in_specs=[pl.BlockSpec(memory_space=pltpu.S...  91.1 us
    pallas_call x2, Pallas kernels, reduce_add(): pl.pallas_call(reduce_kernel, in_specs=[vmem, vmem], out_specs=vmem, out_...  74.4 us
    pallas_call x1, Pallas kernels, expert(): pl.pallas_call(expert_kernel, grid=(ffn // tile,), in_specs=[pl.BlockSpec...  36.1 us
    pallas_call x1, Pallas kernels, project(): pl.pallas_call(project_kernel, grid=(experts,), in_specs=[full(tokens, wi...  15.4 us
    pallas_call x1, Pallas kernels, combine(): pl.pallas_call(combine_kernel, grid=(experts,), in_specs=[full(*o.shape),...  12.9 us
    unnamed x3, local copies, waits for them, and re-layouts  7.87 us

profile of v1, /device:TPU:0, one launch (start us, length us, event | category | flops | bytes accessed | tf_op | source)
XLA Modules:
  0.0 241.1 jit_solution(10125753562283781987)
XLA Ops:
  0.6 0.7 convert_element_type.3
  1.3 1.5 copy.20.ids_ref
  2.9 1.0 fusion
  3.9 1.0 pad_maximum_fusion
  4.9 3.2 %copy.23 = bf16[2048,2,256]{2,0,1:T(8,128)(2,1)} copy(bf16[2048,2,256]{2,1,0:T(2,128)(2,1)} %param.23) | data formatting | bytes 4194304 | tf_op args[7]
  8.0 15.4 %project.1 = (f32[2048,128]{1,0:T(8,128)}, f32[1024,128]{1,0:T(8,128)}, f32[1024,128]{1,0:T(8,128)}, f32[512,8]{1,0:T(8,128)}) custom-call(bf16[512,2048]{1,0:T(8,128)(2,1)} %base_ref.1, f32[1,2048]{1,0:T(1,128)} %bitcast.19, bf16[8,2048]{1,0:T(8,128)(2,1)} %bitcast.16, s32[512,2]{1,0:T(8,128)} %copy.20.ids_ref, f32[512,128]{1,0:T(8,128)} %get-tuple-element.20.cos_ref, ...), custom_call_target="tpu_custom_call" | custom-call | tf_op jit(solution)/shard_map/project/pallas_call | solution.py:69
  23.4 91.1 %attend.1 = (f32[2048,128]{1,0:T(8,128)}, bf16[512,128,128]{2,1,0:T(8,128)(2,1)}, bf16[512,128,128]{2,1,0:T(8,128)(2,1)}) custom-call(s32[512]{0:T(512)} %pos_ref.1, f32[2048,128]{1,0:T(8,128)} %get-tuple-element.10.q_ref, f32[1024,128]{1,0:T(8,128)} %get-tuple-element.11.kn_ref, f32[1024,128]{1,0:T(8,128)} %get-tuple-element.12.vn_ref, ...), custom_call_target="tpu_custom_call" | custom-call | tf_op jit(solution)/shard_map/attend/pallas_call | solution.py:176
  114.5 12.9 %combine.1.part_ref = bf16[512,2048]{1,0:T(8,128)(2,1)} custom-call(f32[2048,128]{1,0:T(8,128)} %get-tuple-element.13.o_ref, s32[512,2]{1,0:T(8,128)} %copy.20.ids_ref, f32[512,8]{1,0:T(8,128)} %get-tuple-element.14.gate_ref, bf16[8,256,2048]{2,1,0:T(8,128)(2,1)} %w_ref.1), custom_call_target="tpu_custom_call" | custom-call | tf_op jit(solution)/shard_map/combine/pallas_call | solution.py:221
  127.4 37.8 %reduce_0.1.x_ref.base_ref = bf16[512,2048]{1,0:T(8,128)(2,1)} custom-call(bf16[512,2048]{1,0:T(8,128)(2,1)} %combine.1.part_ref, bf16[512,2048]{1,0:T(8,128)(2,1)} %base_ref.1), custom_call_target="tpu_custom_call" | custom-call | tf_op jit(solution)/shard_map/reduce_0/pallas_call | solution.py:298
  165.2 36.1 %expert.1.part_ref = bf16[512,2048]{1,0:T(8,128)(2,1)} custom-call(s32[1]{0:T(128)} %bitcast.first_ref, bf16[512,2048]{1,0:T(8,128)(2,1)} %reduce_0.1.x_ref.base_ref, f32[1,2048]{1,0:T(1,128)} %bitcast.18, bf16[8,2048]{1,0:T(8,128)(2,1)} %bitcast.17, s32[2,512]{1,0:T(2,128)} %bitcast.20, bf16[1,2048,5632]{2,1,0:T(8,128)(2,1)} %wg_ref.1, ...), custom_call_target="tpu_custom_call" | custom-call | tf_op jit(solution)/shard_map/expert/pallas_call | solution.py:376
  201.4 36.5 %reduce_1.1 = bf16[512,2048]{1,0:T(8,128)(2,1)} custom-call(bf16[512,2048]{1,0:T(8,128)(2,1)} %expert.1.part_ref, bf16[512,2048]{1,0:T(8,128)(2,1)} %reduce_0.1.x_ref.base_ref), custom_call_target="tpu_custom_call" | custom-call | tf_op jit(solution)/shard_map/reduce_1/pallas_call | solution.py:298
  237.9 3.2 %copy.25 = bf16[512,2048]{1,0:T(8,128)(2,1)} copy(bf16[512,2048]{1,0:T(8,128)(2,1)} %reduce_1.1) | data formatting | bytes 4194304
  (1 shorter events, 0.0 us)
